TPU v7x, 32 devices: a whole 2x2x4 slice. The times are simulated.
32 devices in a mesh: grp: 4 (over y, x), slab: 8 (over z, core).
Axes of the slice: x: 2, y: 2, z: 4, core: 2. Of those that a mesh axis runs over, the one named last changes fastest.
Arguments:
- velocity: float32 [16, 3, 4, 16384], P(None, None, 'grp', 'slab'), may hold values from -6 to 6
- old_basis: bfloat16 [64, 3, 4, 16384], P(None, None, None, 'slab'), may hold values from -6 to 6
- singular_values: float32 [64], replicated, may hold values from 0.7 to 1.4
- thickness: int32 [4, 8], P('grp', 'slab'), may hold values from 1 to 4, as said below
Outputs:
- gram_matrix: float32 [80, 80], replicated
- new_basis: bfloat16 [64, 3, 4, 16384], P(None, None, None, 'slab')
- offsets: int32 [4, 8], P('grp', 'slab')
Inputs may be any that keep to these rules, and one draw needn't show every extreme that they name: `thickness`: the entry at row-major position p differs from 1 + (p * 3) // 32 by at most one. The first entry is 1 and the last is 4.
All inputs are finite; a program needn't handle non-finite values.
Results may differ from a plain program's by a relative error of at most 0.0004.
The roundings to bfloat16 on the way count: a program that leaves them out, or rounds other values in their place, can miss the bound.
Values may be sent and summed in bfloat16 or wider, within the bound.
A program may use at most 64 MiB of HBM per device.

v0:
```python
import jax
import jax.numpy as jnp
from jax import lax
from jax.sharding import PartitionSpec as P

PLANE = 512


def entering(value, axis, join, neutral):
    count, mine = (lax.axis_size(axis), lax.axis_index(axis))
    pieces = lax.all_gather(value, axis)
    total = jnp.full_like(value, 0) + jnp.asarray(neutral, value.dtype)

    def step(position, total):
        longer = join(total, pieces[position])
        return jnp.where(position < mine, longer, total)

    return lax.fori_loop(0, count - 1, step, total)


def orthonormalize(matrix, rank_count):
    iterate = matrix * (0.5 * rank_count**0.5 / jnp.sqrt(jnp.sum(matrix * matrix)))
    for sweep_index in range(4):
        product = jnp.dot(iterate.T, iterate, precision=lax.Precision.HIGHEST)
        iterate = 1.5 * iterate - 0.5 * jnp.dot(iterate, product, precision=lax.Precision.HIGHEST)
    return iterate


def add_counts(earlier, later):
    return earlier + later


def per_device(velocity, old_basis, singular_values, thickness):
    capacity = velocity.shape[-1]
    snap_count = velocity.shape[0]
    rank_count = old_basis.shape[0]
    plane_ids = lax.broadcasted_iota(jnp.int32, (1, capacity), 1) // PLANE
    own_mask = plane_ids < thickness
    masked = jnp.where(
        own_mask[None, None], velocity.astype(jnp.bfloat16), jnp.zeros((), jnp.bfloat16)
    )
    live_cells = lax.psum(jnp.sum(thickness).astype(jnp.float32) * PLANE, ("grp", "slab"))
    region_index = lax.axis_index("grp")
    own_basis = lax.dynamic_slice_in_dim(old_basis, region_index, 1, 2)
    columns = jnp.where(own_mask[None, None], own_basis, jnp.zeros((), jnp.bfloat16))
    stacked = jnp.concatenate([columns.reshape(rank_count, -1), masked.reshape(snap_count, -1)], 0)
    raw_gram = lax.dot_general(
        stacked, stacked, (((1,), (1,)), ((), ())), preferred_element_type=jnp.float32
    )
    partial_terms = (raw_gram,)
    summed = lax.psum((partial_terms[0],), ("grp", "slab"))
    scales = jnp.concatenate([singular_values, jnp.ones((snap_count,), jnp.float32)])
    gram_matrix = summed[0] * scales[:, None] * scales[None, :] / (3.0 * live_cells)
    mixing = orthonormalize(gram_matrix[:, :rank_count], rank_count)
    mixing_rows = (mixing * scales[:, None]).T.astype(jnp.bfloat16)
    updated = jnp.dot(mixing_rows, stacked, preferred_element_type=jnp.float32).astype(jnp.bfloat16)
    new_basis = lax.all_gather(
        updated.reshape(rank_count, 3, 1, capacity), "grp", axis=2, tiled=True
    )
    offsets = entering(thickness, ("grp", "slab"), add_counts, jnp.zeros_like(thickness))
    return (gram_matrix, new_basis, offsets)


def solution(mesh):
    in_specs = (P(None, None, "grp", "slab"), P(None, None, None, "slab"), P(), P("grp", "slab"))
    out_specs = (P(), P(None, None, None, "slab"), P("grp", "slab"))
    return jax.shard_map(
        per_device, mesh=mesh, in_specs=in_specs, out_specs=out_specs, check_vma=False
    )
```

profile of v0, /device:TPU:0, one launch (start us, length us, event | category | flops | bytes accessed | tf_op | source)
XLA Modules:
  0.0 160.7 jit_solution(7786227598539404116)
XLA Ops:
  7.9 2.2 %fusion.7 = bf16[16,3,2048]{2,1,0:T(4,128)(2,1)S(1)} fusion(pred[2048]{0:T(1024)(128)(4,1)S(1)} %fusion.11, f32[16,3,1,2048]{3,2,1,0:T(1,128)} %param.6), kind=kLoop, calls=%fused_computation.15 | loop fusion | flops 196608 | bytes 591872 | tf_op jit(solution)/shard_map/jit(_where)/select_n | solution.py:39
  10.3 7.4 %fusion = bf16[64,3,2048]{2,1,0:T(4,128)(2,1)S(1)} fusion(pred[2048]{0:T(1024)(128)(4,1)S(1)} %fusion.11, bf16[64,3,4,2048]{3,2,1,0:T(4,128)(2,1)} %param.7, s32[]{:T(128)S(6)} %select_n.42), kind=kLoop, calls=%fused_computation.3 | loop fusion | flops 393216 | bytes 1574916 | tf_op jit(solution)/shard_map/jit(_where)/select_n | solution.py:45
  17.7 0.6 copy.29
  19.0 42.7 %all-reduce.2 = (f32[80,80]{1,0:T(8,128)S(1)}, f32[]{:T(128)}) all-reduce(f32[80,80]{1,0:T(8,128)S(1)} %fusion.15, f32[]{:T(128)S(6)} %mul.67), channel_id=1, replica_groups=mesh['grp'=4,'slab'=8] {'grp','slab'}, use_global_device_ids=true, to_apply=%region_0.1 | all-reduce | flops 6401 | bytes 51208 | tf_op jit(solution)/shard_map/psum | solution.py:51
  62.4 0.6 multiply_reduce_fusion
  65.8 1.2 reshape.69
  67.0 1.5 copy.21
  68.5 41.1 %all-reduce.1 = s32[32]{0:T(128)S(1)} all-reduce(s32[32]{0:T(128)S(1)} %bitcast_dynamic-update-slice_fusion), channel_id=2, replica_groups=mesh['grp'=4,'slab'=8] {'grp','slab'}, use_global_device_ids=true, to_apply=%add.1 | all-reduce | flops 32 | bytes 256
  109.7 37.0 %while.13 = (s32[]{:T(128)}, s32[1,1]{1,0:T(1,128)}, s32[]{:T(128)}, s32[32,1,1]{0,2,1:T(1,128)S(1)}, s32[]{:T(128)}) while((s32[]{:T(128)}, s32[1,1]{1,0:T(1,128)}, s32[]{:T(128)}, s32[32,1,1]{0,2,1:T(1,128)S(1)}, s32[]{:T(128)}) %tuple.42), condition=%wide.region_4.5_spmd, body=%wide.region_3.4_spmd.sunk | while | flops 5 | bytes 115 | solution.py:18
  110.8 0.6 constant_dynamic-slice_fusion.2
  112.0 0.6 constant_dynamic-slice_fusion.2
  113.2 0.6 constant_dynamic-slice_fusion.2
  116.8 0.6 constant_dynamic-slice_fusion.2
  118.0 0.6 constant_dynamic-slice_fusion.2
  119.2 0.6 constant_dynamic-slice_fusion.2
  120.4 0.6 constant_dynamic-slice_fusion.2
  124.0 0.6 constant_dynamic-slice_fusion.2
  125.2 0.6 constant_dynamic-slice_fusion.2
  126.4 0.6 constant_dynamic-slice_fusion.2
  127.6 0.6 constant_dynamic-slice_fusion.2
  128.8 0.6 constant_dynamic-slice_fusion.2
  132.4 0.6 constant_dynamic-slice_fusion.2
  133.6 0.6 constant_dynamic-slice_fusion.2
  146.7 6.0 %copy.23 = bf16[64,3,4,2048]{3,2,1,0:T(4,128)(2,1)} copy(bf16[64,3,4,2048]{3,0,1,2:T(8,128)(2,1)} %all-gather.3.cloned.1.call-done) | data formatting | bytes 6291456
  (42 shorter events, 13.1 us)
Async XLA Ops:
  7.2 139.5 %all-gather.3.cloned.1.call-start = ((), (), s32[]{:S(2)}) async-start(), calls=%async_computation | async-start | bytes 3932160 | tf_op jit(solution)/shard_map/all_gather | solution.py:57
  18.3 0.7 copy-start.1
  62.4 4.6 %copy-start = (f32[80,80]{1,0:T(8,128)}, f32[80,80]{1,0:T(8,128)S(1)}, u32[]{:S(2)}) copy-start(f32[80,80]{1,0:T(8,128)S(1)} %multiply_divide_fusion) | copy-start | bytes 76804
Sparse Core Ops, SparseCore 0:
  68.6 44.5 all-gather.2
where the time goes:
time: 161 us
  blocking collectives  83.8 us (52%)
  local copies, waits for them, and re-layouts  27.9 us (17%)
  loops' own time  18.8 us (12%)
  between operations  17.3 us (11%)
  other arithmetic  10.3 us (6%)
  matrix products  2.43 us (2%)
    psum x1, blocking collectives, per_device(): summed = lax.psum((partial_terms[0],), ('grp', 'slab'))  42.7 us
    unnamed x1, blocking collectives  41.1 us
    another operation x1, loops' own time, entering(): return lax.fori_loop(0, count - 1, step, total)  18.8 us
    dynamic_slice x31, local copies, waits for them, and re-layouts, step(): longer = join(total, pieces[position])  18.3 us
    select_n x1, other arithmetic, per_device(): jnp.where(own_mask[None, None], own_basis, jnp.zeros((), jnp.bfloat16))  7.39 us
    unnamed x10, local copies, waits for them, and re-layouts  7.03 us
  transfers between devices with their start and end apart: 1, of which 0 were waited for; matrix products, arithmetic and copies ran while one was open for 11% of the time, Pallas kernels for 0%

commit v1 on v0

v1 whole, which is shorter than its diff:
```python
import jax
import jax.numpy as jnp
from jax import lax
from jax.sharding import PartitionSpec as P

PLANE = 512
AXES = ("grp", "slab")


def orthonormalize(matrix, rank_count):
    iterate = matrix * (0.5 * rank_count**0.5 / jnp.sqrt(jnp.sum(matrix * matrix)))
    for sweep_index in range(4):
        product = jnp.dot(iterate.T, iterate, precision=lax.Precision.HIGHEST)
        iterate = 1.5 * iterate - 0.5 * jnp.dot(iterate, product, precision=lax.Precision.HIGHEST)
    return iterate


def per_device(velocity, old_basis, singular_values, thickness):
    capacity = velocity.shape[-1]
    snap_count = velocity.shape[0]
    rank_count = old_basis.shape[0]
    n_grp, n_slab = lax.axis_size("grp"), lax.axis_size("slab")
    grp, slab = lax.axis_index("grp"), lax.axis_index("slab")
    plane_ids = lax.broadcasted_iota(jnp.int32, (1, capacity), 1) // PLANE
    own_mask = plane_ids < thickness
    masked = jnp.where(
        own_mask[None, None], velocity.astype(jnp.bfloat16), jnp.zeros((), jnp.bfloat16)
    )
    all_snaps = lax.all_gather(masked, "grp", axis=2, tiled=True)
    own_basis = lax.dynamic_slice_in_dim(old_basis, grp, 1, 2)
    columns = jnp.where(own_mask[None, None], own_basis, jnp.zeros((), jnp.bfloat16))
    stacked = jnp.concatenate([columns.reshape(rank_count, -1), masked.reshape(snap_count, -1)], 0)
    raw_gram = lax.dot_general(
        stacked, stacked, (((1,), (1,)), ((), ())), preferred_element_type=jnp.float32
    )
    flat = lax.broadcasted_iota(jnp.int32, (n_grp * n_slab,), 0)
    mine = grp * n_slab + slab
    onehot = jnp.where(flat == mine, thickness[0, 0], 0).astype(jnp.float32)
    raw_gram, counts = lax.psum((raw_gram, onehot), AXES)
    live_cells = jnp.sum(counts) * PLANE
    offsets = jnp.sum(jnp.where(flat < mine, counts, 0.0)).astype(jnp.int32).reshape(1, 1)
    scales = jnp.concatenate([singular_values, jnp.ones((snap_count,), jnp.float32)])
    gram_matrix = raw_gram * scales[:, None] * scales[None, :] / (3.0 * live_cells)
    mixing = orthonormalize(gram_matrix[:, :rank_count], rank_count)
    mixing_rows = (mixing * scales[:, None]).T.astype(jnp.bfloat16)
    slab_counts = lax.dynamic_slice_in_dim(counts.reshape(n_grp, n_slab), slab, 1, 1)
    live = plane_ids.astype(jnp.float32) < slab_counts
    everything = jnp.concatenate([old_basis, all_snaps], 0)
    updated = jnp.einsum(
        "ri,icgn->rcgn", mixing_rows, everything, preferred_element_type=jnp.float32
    )
    new_basis = jnp.where(live[None, None], updated, 0.0).astype(jnp.bfloat16)
    return (gram_matrix, new_basis, offsets)


def solution(mesh):
    in_specs = (P(None, None, "grp", "slab"), P(None, None, None, "slab"), P(), P("grp", "slab"))
    out_specs = (P(), P(None, None, None, "slab"), P("grp", "slab"))
    return jax.shard_map(
        per_device, mesh=mesh, in_specs=in_specs, out_specs=out_specs, check_vma=False
    )
```

time: 161 us -> 80 us (0.50)
  blocking collectives: 83.8 us -> 54.3 us
  local copies, waits for them, and re-layouts: 27.9 us -> 7.68 us
  loops' own time: 18.8 us -> 0 us
  between operations: 17.3 us -> 4.59 us
    unnamed x1 -> x0, blocking collectives: 41.1 us -> none
    another operation x1 -> x0, loops' own time: 18.8 us -> none  [entering(): return lax.fori_loop(0, count - 1, step, total)]
    dynamic_slice x31 -> x1, local copies, waits for them, and re-layouts: 18.3 us -> 0.19 us  [per_device(): lax.dynamic_slice_in_dim(counts.reshape(n_grp, n_slab), slab, 1, 1)]
    all_gather x0 -> x1, blocking collectives: none -> 14.2 us  [per_device(): all_snaps = lax.all_gather(masked, 'grp', axis=2, tiled=True)]
    psum x1, blocking collectives: 42.7 us -> 40.1 us  [per_device(): raw_gram, counts = lax.psum((raw_gram, onehot), AXES)]
    reshape x2 -> x1, local copies, waits for them, and re-layouts: 2.61 us -> 0.08 us  [per_device(): counts.reshape(n_grp, n_slab)]
  transfers between devices with their start and end apart: 1 -> 0, of which waited for: 0 -> 0; matrix products, arithmetic and copies ran while one was open for 11% -> 0% of each run, Pallas kernels for 0% -> 0%
where the time goes in v1:
time: 80 us; the launch traced here: 79.7 us
  blocking collectives  54.3 us (68%)
  other arithmetic  9.91 us (12%)
  local copies, waits for them, and re-layouts  7.68 us (10%)
  between operations  4.59 us (6%)
  matrix products  3.27 us (4%)
    psum x1, blocking collectives, per_device(): raw_gram, counts = lax.psum((raw_gram, onehot), AXES)  40.1 us
    all_gather x1, blocking collectives, per_device(): all_snaps = lax.all_gather(masked, 'grp', axis=2, tiled=True)  14.2 us
    select_n x1, other arithmetic, per_device(): jnp.where(own_mask[None, None], own_basis, jnp.zeros((), jnp.bfloat16))  7.38 us
    unnamed x10, local copies, waits for them, and re-layouts  6.58 us

profile of v1, /device:TPU:0, one launch (start us, length us, event | category | flops | bytes accessed | tf_op | source)
XLA Modules:
  0.0 79.7 jit_solution(17724249454081683966)
XLA Ops:
  1.3 0.7 concatenate.10
  2.0 1.1 %fusion.18 = bf16[16,3,1,2048]{3,0,2,1:T(8,128)(2,1)S(1)} fusion(f32[16,3,1,2048]{3,2,1,0:T(1,128)} %param.4, pred[2048]{0:T(1024)(128)(4,1)S(1)} %fusion.25), kind=kLoop, calls=%fused_computation.23 | loop fusion | flops 98304 | bytes 591872 | tf_op jit(solution)/shard_map/jit(_where)/select_n | solution.py:26
  3.1 0.2 copy.15
  3.3 0.2 copy.28
  3.4 14.2 %all_gather.3 = bf16[16,3,4,2048]{3,0,2,1:T(8,128)(2,1)} all-gather(bf16[16,3,1,2048]{3,0,2,1:T(8,128)(2,1)S(1)} %fusion.18), channel_id=1, replica_groups=mesh['grp'=4,'slab'=8] {'grp'}, dimensions={2}, use_global_device_ids=true | all-gather | bytes 983040 | tf_op jit(solution)/shard_map/all_gather | solution.py:29
  17.6 7.4 %fusion.6 = bf16[64,3,2048]{2,1,0:T(4,128)(2,1)S(1)} fusion(pred[2048]{0:T(1024)(128)(4,1)S(1)} %fusion.25, bf16[64,3,4,2048]{3,2,1,0:T(4,128)(2,1)} %param.5, s32[]{:T(128)S(6)} %select_n.44), kind=kLoop, calls=%fused_computation.6 | loop fusion | flops 393216 | bytes 1574916 | tf_op jit(solution)/shard_map/jit(_where)/select_n | solution.py:31
  25.0 0.6 copy.27
  25.6 0.4 fusion.14
  26.0 40.1 %all-reduce.1 = (f32[80,80]{1,0:T(8,128)S(1)}, f32[32]{0:T(128)S(1)}) all-reduce(f32[80,80]{1,0:T(8,128)S(1)} %fusion.14, f32[32]{0:T(128)S(1)} %fusion.27), channel_id=1, replica_groups=mesh['grp'=4,'slab'=8] {'grp','slab'}, use_global_device_ids=true, to_apply=%region_0.1 | all-reduce | flops 6432 | bytes 51456 | tf_op jit(solution)/shard_map/psum | solution.py:39
  66.1 0.6 fusion.28
  68.1 0.6 multiply_reduce_fusion
  69.5 0.2 dynamic-slice_reduce_fusion
  69.7 0.1 broadcast_compare_fusion
  69.8 0.2 fusion.19
  70.0 0.2 fusion.11
  70.2 0.2 fusion.31
  70.5 0.2 fusion.10
  70.6 0.2 fusion.32
  70.9 0.2 fusion.9
  71.1 0.2 fusion.33
  71.3 0.2 fusion.13
  71.5 1.7 %copy.19 = bf16[64,3,4,2048]{3,0,2,1:T(8,128)(2,1)S(1)} copy(bf16[64,3,4,2048]{3,2,1,0:T(4,128)(2,1)S(1)} %copy-done) | data formatting | bytes 6291456 | tf_op args[1]
  73.3 1.2 %select_convert_fusion = bf16[64,3,4,2048]{3,0,2,1:T(8,128)(2,1)S(1)} fusion(bf16[80,64,1,1]{1,0,3,2:T(8,128)(2,1)S(1)} %fusion.13, bf16[16,3,4,2048]{3,0,2,1:T(8,128)(2,1)S(1)} %copy-done.1, bf16[64,3,4,2048]{3,0,2,1:T(8,128)(2,1)S(1)} %copy.19, pred[4,2048]{1,0:T(4,128)(4,1)S(1)} %broadcast_compare_fusion), kind=kOutput, calls=%fused_computation | convolution fusion | flops 262668288 | bytes 7096320 | tf_op jit(solution)/shard_map/ri,icgn->rcgn/dot_general | solution.py:49
  74.5 4.1 %copy.21 = bf16[64,3,4,2048]{3,2,1,0:T(4,128)(2,1)} copy(bf16[64,3,4,2048]{3,0,2,1:T(8,128)(2,1)S(1)} %select_convert_fusion) | data formatting | bytes 6291456
  (11 shorter events, 0.2 us)
Async XLA Ops:
  25.0 46.5 %copy-start = (bf16[64,3,4,2048]{3,2,1,0:T(4,128)(2,1)S(1)}, bf16[64,3,4,2048]{3,2,1,0:T(4,128)(2,1)}, u32[]{:S(2)}) copy-start(bf16[64,3,4,2048]{3,2,1,0:T(4,128)(2,1)} %param.5) | copy-start | bytes 9437188
  68.1 5.1 %copy-start.2 = (f32[80,80]{1,0:T(8,128)}, f32[80,80]{1,0:T(8,128)S(1)}, u32[]{:S(2)}) copy-start(f32[80,80]{1,0:T(8,128)S(1)} %multiply_divide_fusion) | copy-start | bytes 76804
  71.5 1.8 %copy-start.1 = (bf16[16,3,4,2048]{3,0,2,1:T(8,128)(2,1)S(1)}, bf16[16,3,4,2048]{3,0,2,1:T(8,128)(2,1)}, u32[]{:S(2)}) copy-start(bf16[16,3,4,2048]{3,0,2,1:T(8,128)(2,1)} %all_gather.3) | copy-start | bytes 2359300

commit v2 on v1

v2 whole, which is shorter than its diff:
```python
import functools
import jax
import jax.numpy as jnp
from jax import lax
from jax.experimental import pallas as pl
from jax.experimental.pallas import tpu as pltpu
from jax.sharding import PartitionSpec as P

PLANE = 512
AXES = ("grp", "slab")
MESH = pl.DeviceIdType.MESH
LANES = 128
COUNT_LANE = 32
HIGHEST = lax.Precision.HIGHEST


def stages_of(n_slab, n_grp):
    found = []
    for axis, size, first in (("slab", n_slab, 2), ("grp", n_grp, 4)):
        base, radix = 1, first
        while base < size:
            radix = min(radix, size // base)
            found.append((axis, base, radix))
            base, radix = base * radix, 4
    return found


def partner(axis, base, radix, shift):
    me = {name: lax.axis_index(name) for name in AXES}
    digit = lax.rem(me[axis] // base, radix)
    other = lax.rem(digit + shift, radix)
    me[axis] = me[axis] + (other - digit) * base
    return tuple(me[name] for name in AXES)


def dot(a, b, dims, precision=None):
    return lax.dot_general(
        a, b, (dims, ((), ())), preferred_element_type=jnp.float32, precision=precision
    )


def iota(shape, dim):
    return lax.broadcasted_iota(jnp.int32, shape, dim)


def gram_kernel(
    n_grp, n_slab, stages,
    thick_ref, sv_ref, snaps_ref, basis_ref,
    gram_ref, mixb_ref, mixs_ref, live_ref, offset_ref, all_ref,
    xb, big, small, *rest,
):
    n_st = len(stages)
    slots = rest[:n_st]
    local_sem, v_send, v_recv, st_send, st_recv = rest[n_st:]
    rank, comps = xb.shape[1], xb.shape[0]
    snap = snaps_ref.shape[1]
    planes = xb.shape[3] // PLANE
    wide = rank * n_grp
    grp, slab = lax.axis_index("grp"), lax.axis_index("slab")

    loads = []
    for c in range(comps):
        load = pltpu.make_async_copy(basis_ref.at[:, c], xb.at[c], local_sem.at[c])
        load.start()
        loads.append(load)
    barrier = pltpu.get_barrier_semaphore()
    greeted = 0
    for axis, base, radix in stages:
        for shift in range(1, radix):
            pl.semaphore_signal(
                barrier, inc=1, device_id=partner(axis, base, radix, shift), device_id_type=MESH
            )
            greeted += 1
    keep = pltpu.make_async_copy(snaps_ref, all_ref.at[grp], local_sem.at[comps])
    keep.start()
    pl.semaphore_wait(barrier, greeted)
    sends = []
    for shift in range(1, n_grp):
        send = pltpu.make_async_remote_copy(
            src_ref=snaps_ref, dst_ref=all_ref.at[grp],
            send_sem=v_send.at[shift - 1], recv_sem=v_recv.at[shift - 1],
            device_id=partner("grp", 1, n_grp, shift), device_id_type=MESH,
        )
        send.start()
        sends.append(send)

    thick = thick_ref[0, 0]
    big[...] = jnp.zeros_like(big)
    small[...] = jnp.zeros_like(small)
    for c in range(comps):
        loads[c].wait()
        for p in range(planes):
            live = jnp.where(p < thick, 1.0, 0.0)
            x = xb[c, :, :, pl.ds(p * PLANE, PLANE)].reshape(wide, PLANE)
            s = snaps_ref[c, :, pl.ds(p * PLANE, PLANE)]
            big[:wide] += live * dot(x, x, ((1,), (1,)))
            big[wide:] += live * dot(s, x, ((1,), (1,)))
            small[...] += live * dot(s, s, ((1,), (1,)))
    pick = jnp.where(iota((rank, wide), 1) == iota((rank, wide), 0) * n_grp + grp, 1.0, 0.0)
    right = dot(big[...], pick, ((1,), (1,)), HIGHEST)
    bb = dot(pick, right[:wide], ((1,), (0,)), HIGHEST)
    sb = right[wide:]
    ss = small[...]
    half, quarter = rank // 2, snap // 2
    rows = half + 2 * quarter
    place = iota((quarter, LANES), 1) - COUNT_LANE
    place = jnp.where(place >= 0, place * quarter + iota((quarter, LANES), 0), -1)
    me = grp * n_slab + slab
    tail = jnp.where(place == me, thick.astype(jnp.float32), 0.0)
    spare = jnp.zeros((quarter, LANES - 2 * snap), jnp.float32)
    tail = tail + jnp.concatenate([ss[:quarter], ss[quarter:], spare], 1)
    total = jnp.concatenate(
        [
            jnp.concatenate([bb[:half], bb[half:]], 1),
            jnp.concatenate([sb[:quarter], sb[quarter:]], 1),
            tail,
        ],
        0,
    )
    sv_row = sv_ref[...]
    eye = iota((rank, rank), 0) == iota((rank, rank), 1)
    sv_col = jnp.sum(jnp.where(eye, sv_row, 0.0), axis=1, keepdims=True)

    at = 0
    for (axis, base, radix), slot in zip(stages, slots):
        digit = lax.rem(lax.axis_index(axis) // base, radix)
        slot[digit] = total
        moves = []
        for shift in range(1, radix):
            move = pltpu.make_async_remote_copy(
                src_ref=slot.at[digit], dst_ref=slot.at[digit],
                send_sem=st_send.at[at], recv_sem=st_recv.at[at],
                device_id=partner(axis, base, radix, shift), device_id_type=MESH,
            )
            move.start()
            moves.append(move)
            at += 1
        for move in moves:
            move.wait()
        total = slot[0]
        for k in range(1, radix):
            total = total + slot[k]

    tail = total[half + quarter :]
    counts = jnp.where(place >= 0, tail, 0.0)
    live_cells = jnp.sum(counts, keepdims=True) * PLANE
    factor = 1.0 / (3.0 * live_cells)
    offset_ref[...] = jnp.sum(jnp.where(place < me, counts, 0.0), keepdims=True).astype(jnp.int32)
    live = jnp.zeros((wide, LANES), jnp.float32)
    region = lax.rem(iota((wide, LANES), 0), n_grp)
    for g in range(n_grp):
        here = jnp.sum(jnp.where(place == g * n_slab + slab, counts, 0.0), keepdims=True)
        live = jnp.where(region == g, here, live)
    live_ref[...] = live

    bb = jnp.concatenate([total[:half, :rank], total[:half, rank:]], 0)
    sb = total[half : half + quarter]
    sb = jnp.concatenate([sb[:, :rank], sb[:, rank:]], 0)
    ss = jnp.concatenate([tail[:, :snap], tail[:, snap : 2 * snap]], 0)
    bb = bb * sv_col * sv_row * factor
    sb = sb * sv_row * factor
    ss = ss * factor
    gram_ref[:rank, :rank] = bb
    gram_ref[rank:, :rank] = sb
    gram_ref[:rank, rank:] = sb.T
    gram_ref[rank:, rank:] = ss
    y = jnp.concatenate([bb, sb], 0)
    y = y * (0.5 * rank**0.5 * lax.rsqrt(jnp.sum(y * y, keepdims=True)))
    for sweep in range(4):
        product = dot(y, y, ((0,), (0,)), HIGHEST)
        y = 1.5 * y - 0.5 * dot(y, product, ((1,), (0,)), HIGHEST)
    yb = (y[:rank] * sv_col).astype(jnp.bfloat16)
    ys = y[rank:].astype(jnp.bfloat16)
    spread = jnp.where(iota((rank, wide), 1) // n_grp == iota((rank, wide), 0), 1.0, 0.0)
    spread = spread.astype(jnp.bfloat16)
    left_b = dot(spread, yb, ((0,), (1,))).astype(jnp.bfloat16)
    both = dot(left_b, spread, ((1,), (0,)))
    same = lax.rem(iota((wide, wide), 0), n_grp) == lax.rem(iota((wide, wide), 1), n_grp)
    mixb_ref[...] = jnp.where(same, both, 0.0).astype(jnp.bfloat16)
    reps = n_grp * snap
    fill = jnp.where(lax.rem(iota((snap, reps), 1), snap) == iota((snap, reps), 0), 1.0, 0.0)
    left_s = dot(spread, ys, ((0,), (1,))).astype(jnp.bfloat16)
    many = dot(left_s, fill.astype(jnp.bfloat16), ((1,), (0,)))
    same = lax.rem(iota((wide, reps), 0), n_grp) == iota((wide, reps), 1) // snap
    mixs_ref[...] = jnp.where(same, many, 0.0).astype(jnp.bfloat16)

    keep.wait()
    for send in sends:
        send.wait()


def update_kernel(live_ref, mixb_ref, mixs_ref, basis_ref, snaps_ref, out_ref):
    rank, _, n_grp, cells = basis_ref.shape
    x = basis_ref[...].reshape(rank * n_grp, cells)
    s = snaps_ref[...].reshape(-1, cells)
    new = dot(mixb_ref[...], x, ((1,), (0,))) + dot(mixs_ref[...], s, ((1,), (0,)))
    p = pl.program_id(1).astype(jnp.float32)
    new = jnp.where(p < live_ref[:, :1], new, 0.0).astype(jnp.bfloat16)
    out_ref[...] = new.reshape(out_ref.shape)


def per_device(velocity, old_basis, singular_values, thickness):
    snap, comps, _, capacity = velocity.shape
    rank, n_grp = old_basis.shape[0], old_basis.shape[2]
    n_slab = lax.axis_size("slab")
    planes = capacity // PLANE
    wide, reps = rank * n_grp, n_grp * snap
    stages = stages_of(n_slab, n_grp)
    moves = sum(radix - 1 for _, _, radix in stages)
    rows = rank // 2 + snap
    snaps = velocity[:, :, 0].astype(jnp.bfloat16).transpose(1, 0, 2)
    vmem = pl.BlockSpec(memory_space=pltpu.VMEM)
    hbm = pl.BlockSpec(memory_space=pl.ANY)
    gram_matrix, mix_b, mix_s, live, offsets, all_snaps = pl.pallas_call(
        functools.partial(gram_kernel, n_grp, n_slab, stages),
        out_shape=(
            jax.ShapeDtypeStruct((rank + snap, rank + snap), jnp.float32),
            jax.ShapeDtypeStruct((wide, wide), jnp.bfloat16),
            jax.ShapeDtypeStruct((wide, reps), jnp.bfloat16),
            jax.ShapeDtypeStruct((wide, LANES), jnp.float32),
            jax.ShapeDtypeStruct((1, 1), jnp.int32),
            jax.ShapeDtypeStruct((n_grp, comps, snap, capacity), jnp.bfloat16),
        ),
        in_specs=[pl.BlockSpec(memory_space=pltpu.SMEM), vmem, vmem, hbm],
        out_specs=(vmem, vmem, vmem, vmem, vmem, hbm),
        scratch_shapes=[
            pltpu.VMEM((comps, rank, n_grp, capacity), jnp.bfloat16),
            pltpu.VMEM((wide + snap, wide), jnp.float32),
            pltpu.VMEM((snap, snap), jnp.float32),
            *[pltpu.VMEM((radix, rows, LANES), jnp.float32) for _, _, radix in stages],
            pltpu.SemaphoreType.DMA((comps + 1,)),
            pltpu.SemaphoreType.DMA((n_grp - 1,)),
            pltpu.SemaphoreType.DMA((n_grp - 1,)),
            pltpu.SemaphoreType.DMA((moves,)),
            pltpu.SemaphoreType.DMA((moves,)),
        ],
        compiler_params=pltpu.CompilerParams(collective_id=0, has_side_effects=True),
        name="gram_exchange",
    )(thickness, singular_values.reshape(1, rank), snaps, old_basis)
    new_basis = pl.pallas_call(
        update_kernel,
        out_shape=jax.ShapeDtypeStruct(old_basis.shape, jnp.bfloat16),
        grid=(comps, planes),
        in_specs=[
            pl.BlockSpec((wide, LANES), lambda c, p: (0, 0)),
            pl.BlockSpec((wide, wide), lambda c, p: (0, 0)),
            pl.BlockSpec((wide, reps), lambda c, p: (0, 0)),
            pl.BlockSpec((rank, 1, n_grp, PLANE), lambda c, p: (0, c, 0, p)),
            pl.BlockSpec((n_grp, 1, snap, PLANE), lambda c, p: (0, c, 0, p)),
        ],
        out_specs=pl.BlockSpec((rank, 1, n_grp, PLANE), lambda c, p: (0, c, 0, p)),
        name="basis_update",
    )(live, mix_b, mix_s, old_basis, all_snaps)
    return (gram_matrix, new_basis, offsets)


def solution(mesh):
    in_specs = (P(None, None, "grp", "slab"), P(None, None, None, "slab"), P(), P("grp", "slab"))
    out_specs = (P(), P(None, None, None, "slab"), P("grp", "slab"))
    return jax.shard_map(
        per_device, mesh=mesh, in_specs=in_specs, out_specs=out_specs, check_vma=False
    )
```

time: 80 us -> 36.8 us (0.46)
  blocking collectives: 54.3 us -> 0 us
  Pallas kernels: 0 us -> 31 us
  other arithmetic: 9.91 us -> 0 us
  local copies, waits for them, and re-layouts: 7.68 us -> 2.41 us
  matrix products: 3.27 us -> 0 us
  between operations: 4.59 us -> 3.04 us
    psum x1 -> x0, blocking collectives: 40.1 us -> none  [per_device(): raw_gram, counts = lax.psum((raw_gram, onehot), AXES)]
    pallas_call x0 -> x2, Pallas kernels: none -> 31 us  [the longest x1 21.4 us: per_device(): pl.pallas_call(functools.partial(gram_kernel, n_grp, n_slab, stages), out...]
    all_gather x1 -> x0, blocking collectives: 14.2 us -> none  [per_device(): all_snaps = lax.all_gather(masked, 'grp', axis=2, tiled=True)]
    select_n x2 -> x0, other arithmetic: 8.52 us -> none  [the longest x1 7.38 us: per_device(): jnp.where(own_mask[None, None], own_basis, jnp.zeros((), jnp.bfloat16))]
    unnamed x10 -> x4, local copies, waits for them, and re-layouts: 6.58 us -> 2.41 us
    dot_general x10 -> x0, matrix products: 3.27 us -> none  [the longest x1 1.22 us: per_device(): jnp.einsum('ri,icgn->rcgn', mixing_rows, everything, preferred_element_ty...]
    reduce_sum x2 -> x0, other arithmetic: 1.21 us -> none  [the longest x1 0.61 us: orthonormalize(): jnp.sum(matrix * matrix)]
where the time goes in v2:
time: 36.8 us; the launch traced here: 36.4 us
  Pallas kernels  31 us (84%)
  between operations  3.04 us (8%)
  local copies, waits for them, and re-layouts  2.41 us (7%)
    pallas_call x1, Pallas kernels, per_device(): pl.pallas_call(functools.partial(gram_kernel, n_grp, n_slab, stages), out...  21.4 us
    pallas_call x1, Pallas kernels, per_device(): pl.pallas_call(update_kernel, out_shape=jax.ShapeDtypeStruct(old_basis.sh...  9.58 us
    unnamed x4, local copies, waits for them, and re-layouts  2.41 us

profile of v2, /device:TPU:0, one launch (start us, length us, event | category | flops | bytes accessed | tf_op | source)
XLA Modules:
  0.0 36.4 jit_solution(11446481816321565639)
XLA Ops:
  1.3 1.8 %copy.11 = bf16[16,3,1,2048]{3,0,1,2:T(8,128)(2,1)} copy(f32[16,3,1,2048]{3,2,1,0:T(1,128)} %param.4) | data formatting | bytes 589824 | tf_op args[0]
  3.1 21.4 %gram_exchange.1 = (f32[80,80]{1,0:T(8,128)}, bf16[256,256]{1,0:T(8,128)(2,1)}, bf16[256,64]{1,0:T(8,128)(2,1)}, f32[256,128]{1,0:T(8,128)}, s32[1,1]{1,0:T(1,128)}, /*index=5*/bf16[4,3,16,2048]{3,2,1,0:T(8,128)(2,1)}) custom-call(s32[1,1]{1,0:T(1,128)S(6)} %copy.14.thick_ref, f32[1,64]{1,0:T(1,128)} %bitcast.7, bf16[3,16,2048]{2,1,0:T(8,128)(2,1)} %bitcast.6, ...), custom_call_target="tpu_custom_call" | custom-call | tf_op jit(solution)/shard_map/gram_exchange/pallas_call | solution.py:214
  24.5 0.0 copy-start
  24.5 9.6 %basis_update.1 = bf16[64,3,4,2048]{3,2,1,0:T(4,128)(2,1)} custom-call(f32[256,128]{1,0:T(8,128)} %get-tuple-element.10.live_ref, bf16[256,256]{1,0:T(8,128)(2,1)} %get-tuple-element.11.mixb_ref, bf16[256,64]{1,0:T(8,128)(2,1)} %get-tuple-element.12.mixs_ref, bf16[64,3,4,2048]{3,2,1,0:T(4,128)(2,1)} %basis_ref.3, ...), custom_call_target="tpu_custom_call" | custom-call | tf_op jit(solution)/shard_map/basis_update/pallas_call | solution.py:240
  34.1 0.0 copy-done
  34.1 0.6 %copy.15 = f32[80,80]{1,0:T(8,128)} copy(f32[80,80]{1,0:T(8,128)S(1)} %copy-done) | data formatting | bytes 51200
Async XLA Ops:
  24.5 9.6 %copy-start = (f32[80,80]{1,0:T(8,128)S(1)}, f32[80,80]{1,0:T(8,128)}, u32[]{:S(2)}) copy-start(f32[80,80]{1,0:T(8,128)} %get-tuple-element.18) | copy-start | bytes 76804

commit v3 on v2

--- a/solution.py
+++ b/solution.py
@@ -45,9 +45,9 @@
 
 def gram_kernel(
     n_grp, n_slab, stages,
-    thick_ref, sv_ref, snaps_ref, basis_ref,
+    thick_ref, sv_ref, vel_ref, basis_ref,
     gram_ref, mixb_ref, mixs_ref, live_ref, offset_ref, all_ref,
-    xb, big, small, *rest,
+    xb, snaps_ref, big, small, *rest,
 ):
     n_st = len(stages)
     slots = rest[:n_st]
@@ -71,18 +71,26 @@
                 barrier, inc=1, device_id=partner(axis, base, radix, shift), device_id_type=MESH
             )
             greeted += 1
+    for c in range(comps):
+        snaps_ref[c] = vel_ref[:, c, 0, :].astype(jnp.bfloat16)
     keep = pltpu.make_async_copy(snaps_ref, all_ref.at[grp], local_sem.at[comps])
     keep.start()
     pl.semaphore_wait(barrier, greeted)
     sends = []
-    for shift in range(1, n_grp):
-        send = pltpu.make_async_remote_copy(
-            src_ref=snaps_ref, dst_ref=all_ref.at[grp],
-            send_sem=v_send.at[shift - 1], recv_sem=v_recv.at[shift - 1],
-            device_id=partner("grp", 1, n_grp, shift), device_id_type=MESH,
-        )
-        send.start()
-        sends.append(send)
+
+    def send_snaps(c):
+        for shift in range(1, n_grp):
+            at = c * (n_grp - 1) + shift - 1
+            send = pltpu.make_async_remote_copy(
+                src_ref=snaps_ref.at[c], dst_ref=all_ref.at[grp, c],
+                send_sem=v_send.at[at], recv_sem=v_recv.at[at],
+                device_id=partner("grp", 1, n_grp, shift), device_id_type=MESH,
+            )
+            send.start()
+            sends.append(send)
+
+    for c in range(comps - 1):
+        send_snaps(c)
 
     thick = thick_ref[0, 0]
     big[...] = jnp.zeros_like(big)
@@ -93,13 +101,20 @@
             live = jnp.where(p < thick, 1.0, 0.0)
             x = xb[c, :, :, pl.ds(p * PLANE, PLANE)].reshape(wide, PLANE)
             s = snaps_ref[c, :, pl.ds(p * PLANE, PLANE)]
-            big[:wide] += live * dot(x, x, ((1,), (1,)))
-            big[wide:] += live * dot(s, x, ((1,), (1,)))
+            by_basis = live * dot(x, x, ((1,), (1,)))
+            by_snaps = live * dot(s, x, ((1,), (1,)))
+            for h in range(wide // LANES):
+                big[h, :wide] += by_basis[:, h * LANES : (h + 1) * LANES]
+                big[h, wide:] += by_snaps[:, h * LANES : (h + 1) * LANES]
             small[...] += live * dot(s, s, ((1,), (1,)))
     pick = jnp.where(iota((rank, wide), 1) == iota((rank, wide), 0) * n_grp + grp, 1.0, 0.0)
-    right = dot(big[...], pick, ((1,), (1,)), HIGHEST)
-    bb = dot(pick, right[:wide], ((1,), (0,)), HIGHEST)
-    sb = right[wide:]
+    mine = [
+        jnp.concatenate([big[h, pl.ds(grp, rank, stride=n_grp), :], big[h, wide:]], 0)
+        for h in range(wide // LANES)
+    ]
+    mine = jnp.concatenate(mine, 1)
+    right = dot(mine, pick, ((1,), (1,)), HIGHEST)
+    bb, sb = right[:rank], right[rank:]
     ss = small[...]
     half, quarter = rank // 2, snap // 2
     rows = half + 2 * quarter
@@ -135,6 +150,8 @@
             move.start()
             moves.append(move)
             at += 1
+        if axis == "grp":
+            send_snaps(comps - 1)
         for move in moves:
             move.wait()
         total = slot[0]
@@ -165,7 +182,7 @@
     gram_ref[:rank, rank:] = sb.T
     gram_ref[rank:, rank:] = ss
     y = jnp.concatenate([bb, sb], 0)
-    y = y * (0.5 * rank**0.5 * lax.rsqrt(jnp.sum(y * y, keepdims=True)))
+    y = y * (0.5 * rank**0.5 / jnp.sqrt(jnp.sum(y * y, keepdims=True)))
     for sweep in range(4):
         product = dot(y, y, ((0,), (0,)), HIGHEST)
         y = 1.5 * y - 0.5 * dot(y, product, ((1,), (0,)), HIGHEST)
@@ -189,14 +206,58 @@
         send.wait()
 
 
-def update_kernel(live_ref, mixb_ref, mixs_ref, basis_ref, snaps_ref, out_ref):
-    rank, _, n_grp, cells = basis_ref.shape
-    x = basis_ref[...].reshape(rank * n_grp, cells)
-    s = snaps_ref[...].reshape(-1, cells)
-    new = dot(mixb_ref[...], x, ((1,), (0,))) + dot(mixs_ref[...], s, ((1,), (0,)))
-    p = pl.program_id(1).astype(jnp.float32)
-    new = jnp.where(p < live_ref[:, :1], new, 0.0).astype(jnp.bfloat16)
-    out_ref[...] = new.reshape(out_ref.shape)
+def update_kernel(
+    gram_in, offset_in, live_hbm, mixb_hbm, mixs_hbm, basis_hbm, snaps_hbm,
+    gram_out, offset_out, out_hbm,
+    gram_ref, offset_ref, live_ref, mixb_ref, mixs_ref, xb, sb, ob, sem, in_sem, out_sem,
+):
+    comps, rank, n_grp, capacity = xb.shape
+    snap = sb.shape[2]
+    planes = capacity // PLANE
+    small = []
+    pairs = [(mixb_hbm, mixb_ref), (mixs_hbm, mixs_ref), (live_hbm, live_ref)]
+    pairs += [(gram_in, gram_ref), (offset_in, offset_ref)]
+    for k, (src, dst) in enumerate(pairs):
+        small.append(pltpu.make_async_copy(src, dst, sem.at[k]))
+        small[-1].start()
+    blocks, snap_loads = {}, []
+    for c in range(comps):
+        load = pltpu.make_async_copy(snaps_hbm.at[:, c], sb.at[c], sem.at[len(pairs) + c])
+        load.start()
+        snap_loads.append(load)
+        for p in range(planes):
+            cells = pl.ds(p * PLANE, PLANE)
+            load = pltpu.make_async_copy(
+                basis_hbm.at[:, c, :, cells], xb.at[c, :, :, cells], in_sem.at[c, p]
+            )
+            load.start()
+            blocks[c, p] = load
+    for load in small:
+        load.wait()
+    outs = [
+        pltpu.make_async_copy(gram_ref, gram_out, sem.at[3]),
+        pltpu.make_async_copy(offset_ref, offset_out, sem.at[4]),
+    ]
+    for out in outs:
+        out.start()
+    live = live_ref[:, :1]
+    for c in range(comps):
+        snap_loads[c].wait()
+        for p in range(planes):
+            cells = pl.ds(p * PLANE, PLANE)
+            blocks[c, p].wait()
+            x = xb[c, :, :, cells].reshape(rank * n_grp, PLANE)
+            s = sb[c, :, :, cells].reshape(n_grp * snap, PLANE)
+            new = dot(mixb_ref[...], x, ((1,), (0,))) + dot(mixs_ref[...], s, ((1,), (0,)))
+            new = jnp.where(p < live, new, 0.0).astype(jnp.bfloat16)
+            ob[c, :, :, cells] = new.reshape(rank, n_grp, PLANE)
+            out = pltpu.make_async_copy(
+                ob.at[c, :, :, cells], out_hbm.at[:, c, :, cells], out_sem.at[c, p]
+            )
+            out.start()
+            outs.append(out)
+    for out in outs:
+        out.wait()
 
 
 def per_device(velocity, old_basis, singular_values, thickness):
@@ -208,7 +269,6 @@
     stages = stages_of(n_slab, n_grp)
     moves = sum(radix - 1 for _, _, radix in stages)
     rows = rank // 2 + snap
-    snaps = velocity[:, :, 0].astype(jnp.bfloat16).transpose(1, 0, 2)
     vmem = pl.BlockSpec(memory_space=pltpu.VMEM)
     hbm = pl.BlockSpec(memory_space=pl.ANY)
     gram_matrix, mix_b, mix_s, live, offsets, all_snaps = pl.pallas_call(
@@ -225,32 +285,43 @@
         out_specs=(vmem, vmem, vmem, vmem, vmem, hbm),
         scratch_shapes=[
             pltpu.VMEM((comps, rank, n_grp, capacity), jnp.bfloat16),
-            pltpu.VMEM((wide + snap, wide), jnp.float32),
+            pltpu.VMEM((comps, snap, capacity), jnp.bfloat16),
+            pltpu.VMEM((wide // LANES, wide + snap, LANES), jnp.float32),
             pltpu.VMEM((snap, snap), jnp.float32),
             *[pltpu.VMEM((radix, rows, LANES), jnp.float32) for _, _, radix in stages],
             pltpu.SemaphoreType.DMA((comps + 1,)),
-            pltpu.SemaphoreType.DMA((n_grp - 1,)),
-            pltpu.SemaphoreType.DMA((n_grp - 1,)),
+            pltpu.SemaphoreType.DMA((comps * (n_grp - 1),)),
+            pltpu.SemaphoreType.DMA((comps * (n_grp - 1),)),
             pltpu.SemaphoreType.DMA((moves,)),
             pltpu.SemaphoreType.DMA((moves,)),
         ],
         compiler_params=pltpu.CompilerParams(collective_id=0, has_side_effects=True),
         name="gram_exchange",
-    )(thickness, singular_values.reshape(1, rank), snaps, old_basis)
-    new_basis = pl.pallas_call(
+    )(thickness, singular_values.reshape(1, rank), velocity, old_basis)
+    gram_matrix, offsets, new_basis = pl.pallas_call(
         update_kernel,
-        out_shape=jax.ShapeDtypeStruct(old_basis.shape, jnp.bfloat16),
-        grid=(comps, planes),
-        in_specs=[
-            pl.BlockSpec((wide, LANES), lambda c, p: (0, 0)),
-            pl.BlockSpec((wide, wide), lambda c, p: (0, 0)),
-            pl.BlockSpec((wide, reps), lambda c, p: (0, 0)),
-            pl.BlockSpec((rank, 1, n_grp, PLANE), lambda c, p: (0, c, 0, p)),
-            pl.BlockSpec((n_grp, 1, snap, PLANE), lambda c, p: (0, c, 0, p)),
+        out_shape=(
+            jax.ShapeDtypeStruct(gram_matrix.shape, jnp.float32),
+            jax.ShapeDtypeStruct((1, 1), jnp.int32),
+            jax.ShapeDtypeStruct(old_basis.shape, jnp.bfloat16),
+        ),
+        in_specs=[hbm] * 7,
+        out_specs=(hbm, hbm, hbm),
+        scratch_shapes=[
+            pltpu.VMEM(gram_matrix.shape, jnp.float32),
+            pltpu.VMEM((1, 1), jnp.int32),
+            pltpu.VMEM((wide, LANES), jnp.float32),
+            pltpu.VMEM((wide, wide), jnp.bfloat16),
+            pltpu.VMEM((wide, reps), jnp.bfloat16),
+            pltpu.VMEM((comps, rank, n_grp, capacity), jnp.bfloat16),
+            pltpu.VMEM((comps, n_grp, snap, capacity), jnp.bfloat16),
+            pltpu.VMEM((comps, rank, n_grp, capacity), jnp.bfloat16),
+            pltpu.SemaphoreType.DMA((5 + comps,)),
+            pltpu.SemaphoreType.DMA((comps, planes)),
+            pltpu.SemaphoreType.DMA((comps, planes)),
         ],
-        out_specs=pl.BlockSpec((rank, 1, n_grp, PLANE), lambda c, p: (0, c, 0, p)),
         name="basis_update",
-    )(live, mix_b, mix_s, old_basis, all_snaps)
+    )(gram_matrix, offsets, live, mix_b, mix_s, old_basis, all_snaps)
     return (gram_matrix, new_basis, offsets)
 
 

time: 36.8 us -> 29.2 us (0.79)
  Pallas kernels: 31 us -> 27.7 us
  local copies, waits for them, and re-layouts: 2.41 us -> 0 us
  between operations: 3.04 us -> 1.28 us
    pallas_call x1, Pallas kernels: 9.58 us -> 6.93 us  [per_device(): pl.pallas_call(update_kernel, out_shape=(jax.ShapeDtypeStruct(gram_matrix...]
    unnamed x4 -> x0, local copies, waits for them, and re-layouts: 2.41 us -> none
    pallas_call x1, Pallas kernels: 21.4 us -> 20.8 us  [per_device(): pl.pallas_call(functools.partial(gram_kernel, n_grp, n_slab, stages), out...]
where the time goes in v3:
time: 29.2 us; the launch traced here: 29 us
  Pallas kernels  27.7 us (95%)
  between operations  1.28 us (4%)
    pallas_call x1, Pallas kernels, per_device(): pl.pallas_call(functools.partial(gram_kernel, n_grp, n_slab, stages), out...  20.8 us
    pallas_call x1, Pallas kernels, per_device(): pl.pallas_call(update_kernel, out_shape=(jax.ShapeDtypeStruct(gram_matrix...  6.93 us

profile of v3, /device:TPU:0, one launch (start us, length us, event | category | flops | bytes accessed | tf_op | source)
XLA Modules:
  0.0 29.0 jit_solution(13932972656565411967)
XLA Ops:
  1.3 20.8 %gram_exchange.1 = (f32[80,80]{1,0:T(8,128)}, bf16[256,256]{1,0:T(8,128)(2,1)}, bf16[256,64]{1,0:T(8,128)(2,1)}, f32[256,128]{1,0:T(8,128)}, s32[1,1]{1,0:T(1,128)}, /*index=5*/bf16[4,3,16,2048]{3,2,1,0:T(8,128)(2,1)}) custom-call(s32[1,1]{1,0:T(1,128)S(6)} %copy.7.thick_ref, f32[1,64]{1,0:T(1,128)} %bitcast.1, f32[16,3,1,2048]{3,2,1,0:T(1,128)} %vel_ref.1, ...), custom_call_target="tpu_custom_call" | custom-call | tf_op jit(solution)/shard_map/gram_exchange/pallas_call | solution.py:274
  22.1 6.9 %basis_update.1 = (f32[80,80]{1,0:T(8,128)}, s32[1,1]{1,0:T(1,128)}, bf16[64,3,4,2048]{3,2,1,0:T(4,128)(2,1)}) custom-call(f32[80,80]{1,0:T(8,128)} %get-tuple-element.12.gram_in, s32[1,1]{1,0:T(1,128)} %get-tuple-element.13.offset_in, f32[256,128]{1,0:T(8,128)} %get-tuple-element.14.live_hbm, bf16[256,256]{1,0:T(8,128)(2,1)} %get-tuple-element.15.mixb_hbm, ...), custom_call_target="tpu_custom_call" | custom-call | tf_op jit(solution)/shard_map/basis_update/pallas_call | solution.py:301

commit v4 on v3

--- a/solution.py
+++ b/solution.py
@@ -45,9 +45,9 @@
 
 def gram_kernel(
     n_grp, n_slab, stages,
-    thick_ref, sv_ref, vel_ref, basis_ref,
-    gram_ref, mixb_ref, mixs_ref, live_ref, offset_ref, all_ref,
-    xb, snaps_ref, big, small, *rest,
+    thick_ref, sv_ref, vel_hbm, basis_ref,
+    gram_ref, mixb_ref, mixs_ref, live_ref, offset_ref, all_ref, xb,
+    vel_ref, snaps_ref, big, small, *rest,
 ):
     n_st = len(stages)
     slots = rest[:n_st]
@@ -58,6 +58,8 @@
     wide = rank * n_grp
     grp, slab = lax.axis_index("grp"), lax.axis_index("slab")
 
+    fetch = pltpu.make_async_copy(vel_hbm, vel_ref, local_sem.at[comps + 1])
+    fetch.start()
     loads = []
     for c in range(comps):
         load = pltpu.make_async_copy(basis_ref.at[:, c], xb.at[c], local_sem.at[c])
@@ -71,11 +73,11 @@
                 barrier, inc=1, device_id=partner(axis, base, radix, shift), device_id_type=MESH
             )
             greeted += 1
+    fetch.wait()
     for c in range(comps):
         snaps_ref[c] = vel_ref[:, c, 0, :].astype(jnp.bfloat16)
     keep = pltpu.make_async_copy(snaps_ref, all_ref.at[grp], local_sem.at[comps])
     keep.start()
-    pl.semaphore_wait(barrier, greeted)
     sends = []
 
     def send_snaps(c):
@@ -88,9 +90,6 @@
             )
             send.start()
             sends.append(send)
-
-    for c in range(comps - 1):
-        send_snaps(c)
 
     thick = thick_ref[0, 0]
     big[...] = jnp.zeros_like(big)
@@ -107,6 +106,10 @@
                 big[h, :wide] += by_basis[:, h * LANES : (h + 1) * LANES]
                 big[h, wide:] += by_snaps[:, h * LANES : (h + 1) * LANES]
             small[...] += live * dot(s, s, ((1,), (1,)))
+        if c == 0:
+            pl.semaphore_wait(barrier, greeted)
+            for k in range(comps):
+                send_snaps(k)
     pick = jnp.where(iota((rank, wide), 1) == iota((rank, wide), 0) * n_grp + grp, 1.0, 0.0)
     mine = [
         jnp.concatenate([big[h, pl.ds(grp, rank, stride=n_grp), :], big[h, wide:]], 0)
@@ -150,8 +153,6 @@
             move.start()
             moves.append(move)
             at += 1
-        if axis == "grp":
-            send_snaps(comps - 1)
         for move in moves:
             move.wait()
         total = slot[0]
@@ -207,9 +208,9 @@
 
 
 def update_kernel(
-    gram_in, offset_in, live_hbm, mixb_hbm, mixs_hbm, basis_hbm, snaps_hbm,
+    gram_in, offset_in, live_hbm, mixb_hbm, mixs_hbm, snaps_hbm, xb,
     gram_out, offset_out, out_hbm,
-    gram_ref, offset_ref, live_ref, mixb_ref, mixs_ref, xb, sb, ob, sem, in_sem, out_sem,
+    gram_ref, offset_ref, live_ref, mixb_ref, mixs_ref, sb, ob, sem, out_sem,
 ):
     comps, rank, n_grp, capacity = xb.shape
     snap = sb.shape[2]
@@ -220,18 +221,11 @@
     for k, (src, dst) in enumerate(pairs):
         small.append(pltpu.make_async_copy(src, dst, sem.at[k]))
         small[-1].start()
-    blocks, snap_loads = {}, []
+    snap_loads = []
     for c in range(comps):
         load = pltpu.make_async_copy(snaps_hbm.at[:, c], sb.at[c], sem.at[len(pairs) + c])
         load.start()
         snap_loads.append(load)
-        for p in range(planes):
-            cells = pl.ds(p * PLANE, PLANE)
-            load = pltpu.make_async_copy(
-                basis_hbm.at[:, c, :, cells], xb.at[c, :, :, cells], in_sem.at[c, p]
-            )
-            load.start()
-            blocks[c, p] = load
     for load in small:
         load.wait()
     outs = [
@@ -245,7 +239,6 @@
         snap_loads[c].wait()
         for p in range(planes):
             cells = pl.ds(p * PLANE, PLANE)
-            blocks[c, p].wait()
             x = xb[c, :, :, cells].reshape(rank * n_grp, PLANE)
             s = sb[c, :, :, cells].reshape(n_grp * snap, PLANE)
             new = dot(mixb_ref[...], x, ((1,), (0,))) + dot(mixs_ref[...], s, ((1,), (0,)))
@@ -271,7 +264,7 @@
     rows = rank // 2 + snap
     vmem = pl.BlockSpec(memory_space=pltpu.VMEM)
     hbm = pl.BlockSpec(memory_space=pl.ANY)
-    gram_matrix, mix_b, mix_s, live, offsets, all_snaps = pl.pallas_call(
+    gram_matrix, mix_b, mix_s, live, offsets, all_snaps, held = pl.pallas_call(
         functools.partial(gram_kernel, n_grp, n_slab, stages),
         out_shape=(
             jax.ShapeDtypeStruct((rank + snap, rank + snap), jnp.float32),
@@ -280,16 +273,17 @@
             jax.ShapeDtypeStruct((wide, LANES), jnp.float32),
             jax.ShapeDtypeStruct((1, 1), jnp.int32),
             jax.ShapeDtypeStruct((n_grp, comps, snap, capacity), jnp.bfloat16),
+            pltpu.VMEM((comps, rank, n_grp, capacity), jnp.bfloat16),
         ),
-        in_specs=[pl.BlockSpec(memory_space=pltpu.SMEM), vmem, vmem, hbm],
-        out_specs=(vmem, vmem, vmem, vmem, vmem, hbm),
+        in_specs=[pl.BlockSpec(memory_space=pltpu.SMEM), vmem, hbm, hbm],
+        out_specs=(vmem, vmem, vmem, vmem, vmem, hbm, vmem),
         scratch_shapes=[
-            pltpu.VMEM((comps, rank, n_grp, capacity), jnp.bfloat16),
+            pltpu.VMEM(velocity.shape, jnp.float32),
             pltpu.VMEM((comps, snap, capacity), jnp.bfloat16),
             pltpu.VMEM((wide // LANES, wide + snap, LANES), jnp.float32),
             pltpu.VMEM((snap, snap), jnp.float32),
             *[pltpu.VMEM((radix, rows, LANES), jnp.float32) for _, _, radix in stages],
-            pltpu.SemaphoreType.DMA((comps + 1,)),
+            pltpu.SemaphoreType.DMA((comps + 2,)),
             pltpu.SemaphoreType.DMA((comps * (n_grp - 1),)),
             pltpu.SemaphoreType.DMA((comps * (n_grp - 1),)),
             pltpu.SemaphoreType.DMA((moves,)),
@@ -298,6 +292,7 @@
         compiler_params=pltpu.CompilerParams(collective_id=0, has_side_effects=True),
         name="gram_exchange",
     )(thickness, singular_values.reshape(1, rank), velocity, old_basis)
+    held = pltpu.with_memory_space_constraint(held, pltpu.VMEM)
     gram_matrix, offsets, new_basis = pl.pallas_call(
         update_kernel,
         out_shape=(
@@ -305,7 +300,7 @@
             jax.ShapeDtypeStruct((1, 1), jnp.int32),
             jax.ShapeDtypeStruct(old_basis.shape, jnp.bfloat16),
         ),
-        in_specs=[hbm] * 7,
+        in_specs=[hbm] * 6 + [vmem],
         out_specs=(hbm, hbm, hbm),
         scratch_shapes=[
             pltpu.VMEM(gram_matrix.shape, jnp.float32),
@@ -313,15 +308,13 @@
             pltpu.VMEM((wide, LANES), jnp.float32),
             pltpu.VMEM((wide, wide), jnp.bfloat16),
             pltpu.VMEM((wide, reps), jnp.bfloat16),
-            pltpu.VMEM((comps, rank, n_grp, capacity), jnp.bfloat16),
             pltpu.VMEM((comps, n_grp, snap, capacity), jnp.bfloat16),
             pltpu.VMEM((comps, rank, n_grp, capacity), jnp.bfloat16),
             pltpu.SemaphoreType.DMA((5 + comps,)),
             pltpu.SemaphoreType.DMA((comps, planes)),
-            pltpu.SemaphoreType.DMA((comps, planes)),
         ],
         name="basis_update",
-    )(gram_matrix, offsets, live, mix_b, mix_s, old_basis, all_snaps)
+    )(gram_matrix, offsets, live, mix_b, mix_s, all_snaps, held)
     return (gram_matrix, new_basis, offsets)
 
 

time: 29.2 us -> 27.4 us (0.938)
  Pallas kernels: 27.7 us -> 25.9 us
    pallas_call x1, Pallas kernels: 6.93 us -> 4.7 us  [per_device(): pl.pallas_call(update_kernel, out_shape=(jax.ShapeDtypeStruct(gram_matrix...]
    pallas_call x1, Pallas kernels: 20.8 us -> 21.2 us  [per_device(): pl.pallas_call(functools.partial(gram_kernel, n_grp, n_slab, stages), out...]
where the time goes in v4:
time: 27.4 us; the launch traced here: 27.2 us
  Pallas kernels  25.9 us (95%)
  between operations  1.29 us (5%)
    pallas_call x1, Pallas kernels, per_device(): pl.pallas_call(functools.partial(gram_kernel, n_grp, n_slab, stages), out...  21.2 us
    pallas_call x1, Pallas kernels, per_device(): pl.pallas_call(update_kernel, out_shape=(jax.ShapeDtypeStruct(gram_matrix...  4.7 us

profile of v4, /device:TPU:0, one launch (start us, length us, event | category | flops | bytes accessed | tf_op | source)
XLA Modules:
  0.0 27.2 jit_solution(16416598504674101559)
XLA Ops:
  1.3 21.2 %gram_exchange.1 = (f32[80,80]{1,0:T(8,128)}, bf16[256,256]{1,0:T(8,128)(2,1)}, bf16[256,64]{1,0:T(8,128)(2,1)}, f32[256,128]{1,0:T(8,128)}, s32[1,1]{1,0:T(1,12...) custom-call(s32[1,1]{1,0:T(1,128)S(6)} %copy.7.thick_ref, f32[1,64]{1,0:T(1,128)} %bitcast.1, ...), custom_call_target="tpu_custom_call" | custom-call | tf_op jit(solution)/shard_map/gram_exchange/pallas_call | solution.py:267
  22.5 4.7 %basis_update.1 = (f32[80,80]{1,0:T(8,128)}, s32[1,1]{1,0:T(1,128)}, bf16[64,3,4,2048]{3,2,1,0:T(4,128)(2,1)}) custom-call(f32[80,80]{1,0:T(8,128)} %get-tuple-element.13.gram_in, s32[1,1]{1,0:T(1,128)} %get-tuple-element.14.offset_in, f32[256,128]{1,0:T(8,128)} %get-tuple-element.15.live_hbm, bf16[256,256]{1,0:T(8,128)(2,1)} %get-tuple-element.16.mixb_hbm, ...), custom_call_target="tpu_custom_call" | custom-call | tf_op jit(solution)/shard_map/basis_update/pallas_call | solution.py:296
